TPU v7x, 32 devices: a whole 2x2x4 slice. The times are simulated.
32 devices in a mesh: grp: 4 (over z), dev: 8 (over y, x, core).
Axes of the slice: x: 2, y: 2, z: 4, core: 2. Of those that a mesh axis runs over, the one named last changes fastest.
Arguments:
- qkv_weight: bfloat16 [2, 4608, 8192], P(None, ('grp', 'dev')), may hold values from -0.09375 to 0.09375
- gate_up_weight: bfloat16 [2, 4608, 73728], P(None, ('grp', 'dev')), may hold values from -0.09375 to 0.09375
- head_slot: int32 [64], replicated, may hold values from 0 to 63, each once
- layer_ids: int32 [2], replicated, may hold values from 0 to 45
- stored_qkv: int32 [46, 64], replicated, may hold values from -16384 to 16383
- stored_gate_up: int32 [46, 576], replicated, may hold values from -16384 to 16383
Outputs:
- served_qkv: bfloat16 [2, 4608, 8192], P(None, 'grp', 'dev')
- served_gate_up: bfloat16 [2, 4608, 73728], P(None, 'grp', 'dev')
- qkv_mismatch: float32 [2, 64], P(None, 'dev')
- gate_up_mismatch: float32 [2, 576], P(None, 'dev')
Inputs may be any that keep to these rules, and one draw needn't show every extreme that they name: `head_slot`: each of the 64 heads appears once.
All inputs are finite; a program needn't handle non-finite values.
Results may differ from a plain program's by a relative error of at most 0.0004.
Values may be sent and summed in bfloat16 or wider, within the bound.
A program may use at most 256 MiB of HBM per device.

v0:
```python
import jax
import jax.numpy as jnp
from jax import lax
from jax.sharding import PartitionSpec as P

HEAD_DIM = 128
FF = 36864
STORED = 46
BLK = 128
NHEAD = 64


stored_unit = 1.0 / 1024.0


def finish(pieces):
    qkv_piece, gate_piece = pieces
    count = qkv_piece.shape[0]
    height = qkv_piece.shape[1]
    served_qkv = qkv_piece.reshape(count, height, qkv_piece.shape[4])
    served_gate = gate_piece.reshape(count, height, 2 * gate_piece.shape[4])
    return (served_qkv, served_gate)


def body(qkv_weight, gate_up_weight, head_slot, layer_ids, stored_qkv, stored_gate_up):
    owners = lax.axis_size("dev")
    owner = lax.axis_index("dev")
    layers = qkv_weight.shape[0]
    rows = qkv_weight.shape[1]
    slots = NHEAD // owners
    width = FF // owners
    blocks = width // BLK
    ordered = qkv_weight.reshape(layers, rows, NHEAD, HEAD_DIM)[:, :, head_slot, :]
    qkv_split = ordered.reshape(layers, rows, 1, owners, slots * HEAD_DIM)
    gate_split = gate_up_weight.reshape(layers, rows, 2, owners, width)
    moved = (
        lax.all_to_all(qkv_split, "dev", split_axis=3, concat_axis=1, tiled=True),
        lax.all_to_all(gate_split, "dev", split_axis=3, concat_axis=1, tiled=True),
    )
    results = finish(moved)
    served_qkv = results[0]
    served_gate = results[1]
    head_part = jnp.sum(ordered.astype(jnp.float32), axis=(1, 3))
    block_part = jnp.sum(
        gate_split.astype(jnp.float32).reshape(layers, rows, 2, owners, blocks, BLK), axis=(1, 5)
    )
    block_part = block_part.transpose(0, 2, 1, 3).reshape(layers, owners * 2 * blocks)
    head_all, block_all = lax.psum((head_part, block_part), ("grp", "dev"))
    head_sum = lax.dynamic_slice_in_dim(head_all, owner * slots, slots, 1)
    block_sum = lax.dynamic_slice_in_dim(block_all, owner * 2 * blocks, 2 * blocks, 1)
    layer_pick = (layer_ids[:, None] == jnp.arange(STORED, dtype=jnp.int32)[None, :]).astype(
        jnp.float32
    )
    picked_qkv = jnp.dot(
        layer_pick,
        stored_qkv.astype(jnp.float32),
        precision=lax.Precision.HIGHEST,
        preferred_element_type=jnp.float32,
    )
    picked_gate = jnp.dot(
        layer_pick,
        stored_gate_up.astype(jnp.float32),
        precision=lax.Precision.HIGHEST,
        preferred_element_type=jnp.float32,
    )
    own_heads = lax.dynamic_slice_in_dim(head_slot, owner * slots, slots, 0)
    picked_qkv = picked_qkv[:, own_heads]
    picked_gate = (
        picked_gate.reshape(layers, 2, owners, blocks)
        .transpose(0, 2, 1, 3)
        .reshape(layers, owners * 2 * blocks)
    )
    picked_gate = lax.dynamic_slice_in_dim(picked_gate, owner * 2 * blocks, 2 * blocks, 1)
    qkv_mismatch = head_sum - picked_qkv * stored_unit
    gate_up_mismatch = block_sum - picked_gate * stored_unit
    return (served_qkv, served_gate, qkv_mismatch, gate_up_mismatch)


def solution(mesh):
    placed = (P(None, ("grp", "dev"), None), P(None, ("grp", "dev"), None), P(), P(), P(), P())
    return jax.shard_map(
        body,
        mesh=mesh,
        in_specs=placed,
        out_specs=(P(None, "grp", "dev"), P(None, "grp", "dev"), P(None, "dev"), P(None, "dev")),
        check_vma=False,
    )
```

profile of v0, /device:TPU:0, one launch (start us, length us, event | category | flops | bytes accessed | tf_op | source)
XLA Modules:
  0.0 738.6 jit_solution(3566983164668967660)
XLA Ops:
  0.6 0.7 compare_select_fusion.1
  1.3 5.3 copy_bitcast_fusion
  6.6 5.7 gather_fusion
  12.3 6.3 copy.34
  18.6 8.2 %reshape.39 = bf16[2,144,1,8,1024]{4,3,1,0,2:T(8,128)(2,1)} reshape(bf16[2,144,64,128]{3,2,1,0:T(8,128)(2,1)} %copy.34) | data formatting | bytes 9437184 | tf_op jit(solution)/shard_map/reshape | solution.py:34
  26.8 7.1 copy.35
  33.9 5.2 all-to-all-start
  39.1 29.1 %copy.45 = bf16[36,8,16,4608]{3,2,1,0:T(8,128)(2,1)} copy(bf16[36,8,16,4608]{3,1,2,0:T(8,128)(2,1)} %bitcast.27) | data formatting | bytes 84934656
  68.2 59.8 %copy.37 = bf16[2,144,2,8,4608]{4,2,1,0,3:T(2,128)(2,1)} copy(bf16[2,144,2,8,4608]{4,3,2,1,0:T(8,128)(2,1)} %bitcast.28) | data formatting | bytes 84934656 | tf_op jit(solution)/shard_map/reshape | solution.py:35
  128.0 0.0 copy-start
  128.0 0.0 copy-start.1
  128.0 0.0 all-to-all-done
  128.0 8.2 %all-to-all-start.1 = ((bf16[2,144,2,8,4608]{4,2,1,0,3:T(2,128)(2,1)}), bf16[2,144,2,8,4608]{4,2,1,0,3:T(2,128)(2,1)}, u32[]{:S(2)}, u32[]{:S(2)}) async-start(bf16[2,144,2,8,4608]{4,2,1,0,3:T(2,128)(2,1)} %copy.37), calls=%async_computation.1 | async-start | bytes 84934656 | tf_op jit(solution)/shard_map/all_to_all | solution.py:38
  136.2 0.0 copy-done
  136.2 0.0 copy-done.1
  136.2 0.2 fusion
  136.4 0.1 reshape.44
  136.6 0.1 reshape.45
  136.7 0.0 copy-start.3
  136.7 0.0 copy-start.2
  136.7 14.8 %convert_reduce_fusion = f32[2,73728]{1,0:T(2,128)S(1)} fusion(bf16[2,144,73728]{2,1,0:T(8,128)(2,1)} %param.7), kind=kLoop, calls=%fused_computation.2 | loop fusion | flops 42319872 | bytes 43057152 | tf_op jit(solution)/shard_map/reduce_sum | solution.py:44
  151.5 0.5 reduce_sum.27
  152.0 0.2 reduce_sum.28
  152.2 0.1 reshape.43
  152.3 0.0 copy-done.3
  152.3 0.1 compare_select_fusion
  152.4 0.0 copy-done.2
  152.4 0.2 fusion.2
  152.7 0.6 gather_fusion.1
  153.2 3.1 convert_reduce_fusion.1
  156.4 473.4 %all-reduce = (f32[2,64]{0,1:T(8,128)S(1)}, f32[2,576]{1,0:T(2,128)S(1)}) all-reduce(f32[2,64]{0,1:T(8,128)S(1)} %convert_reduce_fusion.1, f32[2,576]{1,0:T(2,128)S(1)} %reshape.43), channel_id=1, replica_groups=mesh['grp'=4,'dev'=8] {'grp','dev'}, use_global_device_ids=true, to_apply=%region_1.0 | all-reduce | flops 1280 | bytes 10240 | tf_op jit(solution)/shard_map/psum | solution.py:48
  629.8 0.6 copy.42
  630.4 0.6 multiply_subtract_fusion
  631.1 5.2 copy.36
  636.3 0.0 all-to-all-done.1
  636.3 36.7 %copy.38 = bf16[2,8,144,2,1,4608]{5,3,2,1,0,4:T(2,128)(2,1)} copy(bf16[2,8,144,2,1,4608]{5,3,2,0,1,4:T(2,128)(2,1)} %bitcast.5) | data formatting | bytes 84934656 | tf_op jit(solution)/shard_map/all_to_all | solution.py:38
  673.0 65.6 %reshape.42 = bf16[2,1152,9216]{2,1,0:T(8,128)(2,1)} reshape(bf16[2,8,144,2,1,4608]{5,3,2,1,0,4:T(2,128)(2,1)} %copy.38) | data formatting | bytes 84934656 | tf_op jit(solution)/shard_map/reshape | solution.py:21
  (5 shorter events, 0.0 us)
Async XLA Ops:
  33.9 94.1 %all-to-all-start = ((bf16[2,144,1,8,1024]{4,1,0,2,3:T(8,128)(2,1)}), bf16[2,144,1,8,1024]{4,1,0,2,3:T(8,128)(2,1)}, u32[]{:S(2)}, u32[]{:S(2)}) async-start(bf16[2,144,1,8,1024]{4,1,0,2,3:T(8,128)(2,1)} %copy.35), calls=%async_computation | async-start | bytes 9437184 | tf_op jit(solution)/shard_map/all_to_all | solution.py:37
  128.0 8.2 %copy-start = (s32[46,576]{1,0:T(8,128)S(1)}, s32[46,576]{1,0:T(8,128)}, u32[]{:S(2)}) copy-start(s32[46,576]{1,0:T(8,128)} %param.11) | copy-start | bytes 317956
  128.0 8.2 %copy-start.1 = (s32[2]{0:T(128)S(1)}, s32[2]{0:T(128)}, u32[]{:S(2)}) copy-start(s32[2]{0:T(128)} %param.9) | copy-start | bytes 28
  128.0 508.3 %all-to-all-start.1 = ((bf16[2,144,2,8,4608]{4,2,1,0,3:T(2,128)(2,1)}), bf16[2,144,2,8,4608]{4,2,1,0,3:T(2,128)(2,1)}, u32[]{:S(2)}, u32[]{:S(2)}) async-start(bf16[2,144,2,8,4608]{4,2,1,0,3:T(2,128)(2,1)} %copy.37), calls=%async_computation.1 | async-start | bytes 84934656 | tf_op jit(solution)/shard_map/all_to_all | solution.py:38
  136.7 15.7 %copy-start.3 = (s32[64]{0:T(128)S(1)}, s32[64]{0:T(128)}, u32[]{:S(2)}) copy-start(s32[64]{0:T(128)} %param.8) | copy-start | bytes 772
  136.7 15.8 %copy-start.2 = (s32[46,64]{1,0:T(8,128)S(1)}, s32[46,64]{1,0:T(8,128)}, u32[]{:S(2)}) copy-start(s32[46,64]{1,0:T(8,128)} %param.10) | copy-start | bytes 35332
where the time goes:
time: 741 us; the launch traced here: 739 us
  blocking collectives  473 us (64%)
  local copies, waits for them, and re-layouts  231 us (31%)
  other arithmetic  19.6 us (3%)
  starting transfers between devices  13.4 us (2%)
    psum x1, blocking collectives, body(): head_all, block_all = lax.psum((head_part, block_part), ('grp', 'dev'))  473 us
    reshape x1, local copies, waits for them, and re-layouts, finish(): served_gate = gate_piece.reshape(count, height, 2 * gate_piece.shape[4])  65.6 us
    reshape x1, local copies, waits for them, and re-layouts, body(): gate_split = gate_up_weight.reshape(layers, rows, 2, owners, width)  59.8 us
    all_to_all x1, local copies, waits for them, and re-layouts, body(): lax.all_to_all(gate_split, 'dev', split_axis=3, concat_axis=1, tiled=True)  36.7 us
    unnamed x10, local copies, waits for them, and re-layouts  29.7 us
    reshape x2, local copies, waits for them, and re-layouts, body(): qkv_split = ordered.reshape(layers, rows, 1, owners, slots * HEAD_DIM)  15.3 us
    reduce_sum x2, other arithmetic, body(): jnp.sum(gate_split.astype(jnp.float32).reshape(layers, rows, 2, owners, b...  15 us
  transfers between devices with their start and end apart: 2, of which 0 were waited for; matrix products, arithmetic and copies ran while one was open for 16% of the time, Pallas kernels for 0%

commit v1 on v0

v1 whole, which is shorter than its diff:
```python
import functools

import jax
import jax.numpy as jnp
from jax import lax
from jax.experimental import pallas as pl
from jax.experimental.pallas import tpu as pltpu
from jax.sharding import PartitionSpec as P

HEAD_DIM = 128
BLK = 128
MESH = pl.DeviceIdType.MESH

stored_unit = 1.0 / 1024.0


def partner(me, k, n):
    out = 0
    bit = 1
    while bit < n:
        mine = lax.rem(lax.div(me, bit), 2)
        out = out + bit * ((1 - mine) if k & bit else mine)
        bit *= 2
    return out


def exchange_kernel(
    groups, owners,
    slot_ref, gate_ref, qkv_ref,
    held_ref, perm_ref, tot_ref,
    own_buf, chunk_buf, q_in, q_out, colsum, part, parts_z, mine_z, parts_d,
    send_sem, recv_sem, own_sem, out_sem, chunk_sem, q_sem, zs_sem, zr_sem, ds_sem, dr_sem,
):
    me = lax.axis_index("dev")
    grp = lax.axis_index("grp")
    layers, rows, total = gate_ref.shape
    ff = total // 2
    width = ff // owners
    blocks = width // BLK
    heads = qkv_ref.shape[2] // HEAD_DIM
    slots = heads // owners

    barrier = pltpu.get_barrier_semaphore()
    for k in range(1, owners):
        pl.semaphore_signal(barrier, inc=1, device_id={"dev": partner(me, k, owners)}, device_id_type=MESH)
    for j in range(1, groups):
        pl.semaphore_signal(barrier, inc=1, device_id={"grp": lax.rem(grp + j, groups)}, device_id_type=MESH)
    pl.semaphore_wait(barrier, owners - 1 + groups - 1)

    def columns(p, owner):
        return pl.ds(pl.multiple_of(p * ff + owner * width, BLK), width)

    def send(k, l, p):
        to = partner(me, k, owners)
        return pltpu.make_async_remote_copy(
            src_ref=gate_ref.at[l, :, columns(p, to)],
            dst_ref=held_ref.at[me, l, :, pl.ds(p * width, width)],
            send_sem=send_sem.at[k, l, p],
            recv_sem=recv_sem.at[k, l, p],
            device_id={"dev": to},
            device_id_type=MESH,
        )

    hops = {k: bin(k >> 1).count("1") for k in range(1, owners)}
    near = sorted((k for k in hops if hops[k] == 1), key=lambda k: (k & 1, k))
    far = sorted((k for k in hops if hops[k] > 1), key=lambda k: (hops[k], k & 1, k))
    cores = [k for k in hops if hops[k] == 0]
    pieces = [(l, p) for l in range(layers) for p in range(2)]
    for l, p in pieces:
        for k in near:
            send(k, l, p).start()
    for l, p in pieces:
        for k in cores:
            send(k, l, p).start()

    own_in = [
        pltpu.make_async_copy(gate_ref.at[l, :, columns(p, me)], own_buf.at[l * 2 + p], own_sem.at[l * 2 + p])
        for l, p in pieces
    ]
    own_out = [
        pltpu.make_async_copy(
            own_buf.at[l * 2 + p], held_ref.at[me, l, :, pl.ds(p * width, width)], out_sem.at[l * 2 + p]
        )
        for l, p in pieces
    ]
    q_store = pltpu.make_async_copy(q_out, perm_ref, q_sem.at[heads])

    def q_load(h):
        source = qkv_ref.at[:, :, pl.ds(pl.multiple_of(h * HEAD_DIM, HEAD_DIM), HEAD_DIM)]
        return pltpu.make_async_copy(source, q_in.at[h], q_sem.at[h])

    def q_start(h, carry):
        q_load(h).start()
        return carry

    def q_wait(h, carry):
        q_load(h).wait()
        return carry
    for copy in own_in:
        copy.start()
    lax.fori_loop(0, heads, q_start, 0)

    per = 2 * layers
    count = owners * per

    def chunk(i, slot):
        owner = i // per
        l = (i % per) // 2
        p = i % 2
        return pltpu.make_async_copy(gate_ref.at[l, :, columns(p, owner)], chunk_buf.at[slot], chunk_sem.at[slot])

    chunk(0, 0).start()
    for copy in own_in:
        copy.wait()
    for copy in own_out:
        copy.start()

    colsum[...] = jnp.zeros_like(colsum)
    part[...] = jnp.zeros_like(part)
    lax.fori_loop(0, heads, q_wait, 0)
    lane8 = lax.broadcasted_iota(jnp.int32, (8, BLK), 1)
    row8 = lax.broadcasted_iota(jnp.int32, (8, BLK), 0)

    def head_step(s, carry):
        owner = s // slots
        j = s % slots
        head = q_in[slot_ref[s]]
        for l in range(layers):
            values = head[l]
            q_out[owner, l, :, pl.ds(pl.multiple_of(j * HEAD_DIM, HEAD_DIM), HEAD_DIM)] = values
            cols = jnp.sum(values.astype(jnp.float32), axis=0, keepdims=True)
            head_sum = jnp.sum(cols, axis=1, keepdims=True)
            here = (lane8 == j) & (row8 == per + l)
            part[owner] += jnp.where(here, jnp.broadcast_to(head_sum, (8, BLK)), 0.0)
        return carry

    lax.fori_loop(0, heads, head_step, 0)

    def sum_step(i, carry):
        slot = i % 2

        @pl.when(i + 1 < count)
        def _():
            chunk(i + 1, (i + 1) % 2).start()

        chunk(i, slot).wait()
        sums = jnp.sum(chunk_buf[slot].astype(jnp.float32), axis=0, keepdims=True)
        colsum[i // per, pl.ds(i % per, 1), :] = sums
        return carry

    lax.fori_loop(0, count, sum_step, 0)

    def block_step(o, carry):
        acc = part[o]
        for b in range(blocks):
            s = jnp.sum(colsum[o, :, b * BLK:(b + 1) * BLK], axis=1, keepdims=True)
            acc = acc + jnp.where(lane8 == b, jnp.broadcast_to(s, (8, BLK)), 0.0)
        part[o] = acc
        return carry

    lax.fori_loop(0, owners, block_step, 0)
    q_store.start()

    across = [
        pltpu.make_async_remote_copy(
            src_ref=part,
            dst_ref=parts_z.at[j - 1],
            send_sem=zs_sem.at[j - 1],
            recv_sem=zr_sem.at[j - 1],
            device_id={"grp": lax.rem(grp + j, groups)},
            device_id_type=MESH,
        )
        for j in range(1, groups)
    ]
    for copy in across:
        copy.start()
    for copy in across:
        copy.wait()
    group_sum = part[...]
    for j in range(groups - 1):
        group_sum = group_sum + parts_z[j]
    mine_z[...] = group_sum

    for k in far:
        for l, p in pieces[:1]:
            send(k, l, p).start()
    along = []
    for k in range(1, owners):
        to = partner(me, k, owners)
        along.append(
            pltpu.make_async_remote_copy(
                src_ref=mine_z.at[to],
                dst_ref=parts_d.at[k - 1],
                send_sem=ds_sem.at[k - 1],
                recv_sem=dr_sem.at[k - 1],
                device_id={"dev": to},
                device_id_type=MESH,
            )
        )
    for copy in along:
        copy.start()
    for l, p in pieces[1:]:
        for k in far:
            send(k, l, p).start()
    for copy in along:
        copy.wait()
    all_sum = mine_z[me]
    for k in range(owners - 1):
        all_sum = all_sum + parts_d[k]
    tot_ref[...] = all_sum

    q_store.wait()
    for copy in own_out:
        copy.wait()
    for k in near + cores + far:
        for l, p in pieces:
            send(k, l, p).wait()


def exchange(head_slot, gate, qkv, groups, owners):
    layers, rows, total = gate.shape
    width = total // 2 // owners
    slots = qkv.shape[2] // HEAD_DIM // owners
    any_space = pl.BlockSpec(memory_space=pl.ANY)
    dma = pltpu.SemaphoreType.DMA
    f32 = jnp.float32
    return pl.pallas_call(
        functools.partial(exchange_kernel, groups, owners),
        name="exchange",
        out_shape=(
            jax.ShapeDtypeStruct((owners, layers, rows, 2 * width), gate.dtype),
            jax.ShapeDtypeStruct((owners, layers, rows, slots * HEAD_DIM), qkv.dtype),
            jax.ShapeDtypeStruct((8, BLK), f32),
        ),
        in_specs=[pl.BlockSpec(memory_space=pltpu.SMEM), any_space, any_space],
        out_specs=(any_space, pl.BlockSpec(memory_space=pltpu.HBM), pl.BlockSpec(memory_space=pltpu.VMEM)),
        scratch_shapes=[
            pltpu.VMEM((2 * layers, rows, width), gate.dtype),
            pltpu.VMEM((2, rows, width), gate.dtype),
            pltpu.VMEM((owners * slots, layers, rows, HEAD_DIM), qkv.dtype),
            pltpu.VMEM((owners, layers, rows, slots * HEAD_DIM), qkv.dtype),
            pltpu.VMEM((owners, 8, width), f32),
            pltpu.VMEM((owners, 8, BLK), f32),
            pltpu.VMEM((groups - 1, owners, 8, BLK), f32),
            pltpu.VMEM((owners, 8, BLK), f32),
            pltpu.VMEM((owners - 1, 8, BLK), f32),
            dma((owners, layers, 2)),
            dma((owners, layers, 2)),
            dma((2 * layers,)),
            dma((2 * layers,)),
            dma((2,)),
            dma((owners * slots + 1,)),
            dma((groups - 1,)),
            dma((groups - 1,)),
            dma((owners - 1,)),
            dma((owners - 1,)),
        ],
        compiler_params=pltpu.CompilerParams(
            collective_id=0, has_side_effects=True, vmem_limit_bytes=48 * 1024 * 1024
        ),
        cost_estimate=pl.CostEstimate(flops=0, bytes_accessed=4 * gate.size, transcendentals=0),
    )(head_slot, gate, qkv)


def place_kernel(in_ref, out_ref):
    out_ref[...] = in_ref[0]


def place(held):
    owners, layers, rows, columns = held.shape
    if rows % 16:
        return held.transpose(1, 0, 2, 3).reshape(layers, owners * rows, columns)
    return pl.pallas_call(
        place_kernel,
        name="place",
        grid=(layers, owners),
        in_specs=[pl.BlockSpec((1, 1, rows, columns), lambda l, s: (s, l, 0, 0))],
        out_specs=pl.BlockSpec((1, rows, columns), lambda l, s: (l, s, 0)),
        out_shape=jax.ShapeDtypeStruct((layers, owners * rows, columns), held.dtype),
        compiler_params=pltpu.CompilerParams(vmem_limit_bytes=40 * 1024 * 1024),
        cost_estimate=pl.CostEstimate(
            flops=0, bytes_accessed=4 * held.size, transcendentals=0
        ),
    )(held)


def body(qkv_weight, gate_up_weight, head_slot, layer_ids, stored_qkv, stored_gate_up):
    groups = lax.axis_size("grp")
    owners = lax.axis_size("dev")
    owner = lax.axis_index("dev")
    layers = qkv_weight.shape[0]
    slots = head_slot.shape[0] // owners
    blocks = gate_up_weight.shape[2] // 2 // owners // BLK
    held, perm, tot = exchange(head_slot, gate_up_weight, qkv_weight, groups, owners)
    moved = lax.all_to_all(perm, "dev", split_axis=0, concat_axis=0, tiled=True)
    served_gate = place(held)
    served_qkv = place(moved)
    block_sum = tot[: 2 * layers, :blocks].reshape(layers, 2 * blocks)
    head_sum = tot[2 * layers : 3 * layers, :slots]
    pick = (layer_ids[:, None] == jnp.arange(stored_qkv.shape[0], dtype=jnp.int32)[None, :])
    own_heads = lax.dynamic_slice_in_dim(head_slot, owner * slots, slots, 0)
    head_pick = own_heads[:, None] == jnp.arange(head_slot.shape[0], dtype=jnp.int32)[None, :]
    rows_qkv = jnp.sum(jnp.where(pick[:, :, None], stored_qkv[None], 0), axis=1)
    picked_qkv = jnp.sum(jnp.where(head_pick[None], rows_qkv[:, None, :], 0), axis=2)
    stored_split = stored_gate_up.reshape(stored_gate_up.shape[0], 2, owners * blocks)
    own_gate = lax.dynamic_slice_in_dim(stored_split, owner * blocks, blocks, 2)
    picked_gate = jnp.sum(jnp.where(pick[:, :, None, None], own_gate[None], 0), axis=1)
    picked_gate = picked_gate.reshape(layers, 2 * blocks)
    qkv_mismatch = head_sum - picked_qkv.astype(jnp.float32) * stored_unit
    gate_up_mismatch = block_sum - picked_gate.astype(jnp.float32) * stored_unit
    return (served_qkv, served_gate, qkv_mismatch, gate_up_mismatch)


def solution(mesh):
    placed = (P(None, ("grp", "dev"), None), P(None, ("grp", "dev"), None), P(), P(), P(), P())
    return jax.shard_map(
        body,
        mesh=mesh,
        in_specs=placed,
        out_specs=(P(None, "grp", "dev"), P(None, "grp", "dev"), P(None, "dev"), P(None, "dev")),
        check_vma=False,
    )
```

time: 741 us -> 539 us (0.73)
  Pallas kernels: 0 us -> 507 us
  blocking collectives: 473 us -> 0 us
  local copies, waits for them, and re-layouts: 231 us -> 3.68 us
  waiting for transfers between devices: 0.01 us -> 18.8 us
  other arithmetic: 19.6 us -> 2.86 us
  starting transfers between devices: 13.4 us -> 4.73 us
    pallas_call x0 -> x3, Pallas kernels: none -> 507 us  [the longest x1 465 us: exchange(): pl.pallas_call(functools.partial(exchange_kernel, groups, owners), name='...]
    psum x1 -> x0, blocking collectives: 473 us -> none  [body(): head_all, block_all = lax.psum((head_part, block_part), ('grp', 'dev'))]
    reshape x8 -> x2, local copies, waits for them, and re-layouts: 146 us -> 0.23 us  [the longest x1 0.15 us: body(): stored_gate_up.reshape(stored_gate_up.shape[0], 2, owners * blocks)]
    all_to_all x2 -> x0, local copies, waits for them, and re-layouts: 42 us -> none  [the longest x1 36.7 us: body(): lax.all_to_all(gate_split, 'dev', split_axis=3, concat_axis=1, tiled=True)]
    unnamed x10 -> x13, local copies, waits for them, and re-layouts: 29.7 us -> 2.94 us
    all_to_all x2 -> x1, waiting for transfers between devices: 0.01 us -> 18.8 us  [body(): moved = lax.all_to_all(perm, 'dev', split_axis=0, concat_axis=0, tiled=True)]
    reduce_sum x3, other arithmetic: 18.2 us -> 1.56 us  [the longest x1 1.29 us: body(): jnp.sum(jnp.where(pick[:, :, None, None], own_gate[None], 0), axis=1)]
    gather x3 -> x0, local copies, waits for them, and re-layouts: 12.6 us -> none  [the longest x2 12 us: body(): qkv_weight.reshape(layers, rows, NHEAD, HEAD_DIM)[:, :, head_slot, :]]
  transfers between devices with their start and end apart: 2 -> 1, of which waited for: 0 -> 1; matrix products, arithmetic and copies ran while one was open for 16% -> 1% of each run, Pallas kernels for 0% -> 6%
where the time goes in v1:
time: 539 us; the launch traced here: 538 us
  Pallas kernels  507 us (94%)
  waiting for transfers between devices  18.8 us (3%)
    pallas_call x1, Pallas kernels, exchange(): pl.pallas_call(functools.partial(exchange_kernel, groups, owners), name='...  465 us
    pallas_call x2, Pallas kernels, place(): pl.pallas_call(place_kernel, name='place', grid=(layers, owners), in_spec...  42.4 us
    all_to_all x1, waiting for transfers between devices, body(): moved = lax.all_to_all(perm, 'dev', split_axis=0, concat_axis=0, tiled=True)  18.8 us
  transfers between devices with their start and end apart: 1, of which 1 were waited for; matrix products, arithmetic and copies ran while one was open for 1% of the time, Pallas kernels for 6%

profile of v1, /device:TPU:0, one launch (start us, length us, event | category | flops | bytes accessed | tf_op | source)
XLA Modules:
  0.0 537.8 jit_solution(9424614991596098735)
XLA Ops:
  0.6 0.0 copy-start.1
  0.6 0.6 copy-done.1
  1.3 464.5 %exchange.1 = (bf16[8,2,144,9216]{3,2,1,0:T(8,128)(2,1)}, bf16[8,2,144,1024]{3,2,1,0:T(8,128)(2,1)S(1)}, f32[8,128]{1,0:T(8,128)S(1)}) custom-call(s32[64]{0:T(128)S(1)} %copy-done.1, bf16[2,144,73728]{2,1,0:T(8,128)(2,1)} %gate_ref.1, bf16[2,144,8192]{2,1,0:T(8,128)(2,1)} %qkv_ref.1), custom_call_target="tpu_custom_call" | custom-call | bytes 84934656 | tf_op jit(solution)/shard_map/exchange/pallas_call | solution.py:227
  465.8 0.0 copy-start
  465.8 2.2 copy-done
  468.0 0.0 copy-start.2
  468.0 0.0 copy-start.5
  468.0 0.0 copy-start.3
  468.0 4.7 all-to-all-start
  472.7 0.0 copy-done.2
  472.8 0.1 dynamic_slice.6
  472.8 0.0 copy-done.5
  472.8 0.1 iota_compare_fusion.1
  472.9 0.1 copy.15
  473.0 0.0 copy-done.3
  473.0 0.1 reshape.80
  473.2 0.1 constant_dynamic-slice_fusion
  473.3 0.1 copy.16
  473.4 1.3 select_reduce_fusion
  474.7 0.1 copy.18
  474.8 0.1 mul.23
  474.9 0.1 reshape.79
  475.0 0.0 copy-start.4
  475.0 32.1 %place.3 = bf16[2,1152,9216]{2,1,0:T(8,128)(2,1)} custom-call(bf16[8,2,144,9216]{3,2,1,0:T(8,128)(2,1)} %get-tuple-element.8.in_ref), custom_call_target="tpu_custom_call" | custom-call | bytes 84934656 | tf_op jit(solution)/shard_map/place/pallas_call | solution.py:273
  507.1 0.6 sub.7
  507.7 0.0 copy-done.4
  507.7 0.1 select_reduce_fusion.1
  507.8 0.1 iota_compare_fusion
  507.9 0.1 select_reduce_fusion.2
  508.0 0.6 multiply_subtract_fusion
  508.6 18.8 %all-to-all-done.in_ref = bf16[8,2,144,1024]{3,2,1,0:T(8,128)(2,1)} async-done(((bf16[8,2,144,1024]{3,2,1,0:T(8,128)(2,1)}), bf16[8,2,144,1024]{3,2,1,0:T(8,128)(2,1)}, u32[]{:S(2)}, u32[]{:S(2)}) %all-to-all-start) | async-done | bytes 4718624 | tf_op jit(solution)/shard_map/all_to_all | solution.py:295
  527.5 10.3 %place.2 = bf16[2,1152,1024]{2,1,0:T(8,128)(2,1)} custom-call(bf16[8,2,144,1024]{3,2,1,0:T(8,128)(2,1)} %all-to-all-done.in_ref), custom_call_target="tpu_custom_call" | custom-call | bytes 9437184 | tf_op jit(solution)/shard_map/place/pallas_call | solution.py:273
  (2 shorter events, 0.0 us)
Async XLA Ops:
  0.6 0.7 copy-start.1
  465.8 2.2 copy-start
  468.0 4.8 copy-start.2
  468.0 4.8 copy-start.5
  468.0 5.0 copy-start.3
  468.0 59.5 %all-to-all-start = ((bf16[8,2,144,1024]{3,2,1,0:T(8,128)(2,1)}), bf16[8,2,144,1024]{3,2,1,0:T(8,128)(2,1)}, u32[]{:S(2)}, u32[]{:S(2)}) async-start(bf16[8,2,144,1024]{3,2,1,0:T(8,128)(2,1)} %copy-done), calls=%async_computation | async-start | bytes 9437184 | tf_op jit(solution)/shard_map/all_to_all | solution.py:295
  475.0 32.7 %copy-start.4 = (s32[46,64]{1,0:T(8,128)S(1)}, s32[46,64]{1,0:T(8,128)}, u32[]{:S(2)}) copy-start(s32[46,64]{1,0:T(8,128)} %param.10) | copy-start | bytes 35332

commit v2 on v1

--- a/solution.py
+++ b/solution.py
@@ -256,26 +256,31 @@
             dma((owners - 1,)),
         ],
         compiler_params=pltpu.CompilerParams(
-            collective_id=0, has_side_effects=True, vmem_limit_bytes=48 * 1024 * 1024
+            collective_id=0, has_side_effects=True, vmem_limit_bytes=62 * 1024 * 1024
         ),
         cost_estimate=pl.CostEstimate(flops=0, bytes_accessed=4 * gate.size, transcendentals=0),
     )(head_slot, gate, qkv)
 
 
 def place_kernel(in_ref, out_ref):
-    out_ref[...] = in_ref[0]
+    rows = in_ref.shape[2]
+    for s in range(in_ref.shape[0]):
+        out_ref[0, s * rows : (s + 1) * rows, :] = in_ref[s, 0]
 
 
 def place(held):
     owners, layers, rows, columns = held.shape
     if rows % 16:
         return held.transpose(1, 0, 2, 3).reshape(layers, owners * rows, columns)
+    at_once = 1
+    while at_once * 2 <= owners // 2 and at_once * rows * columns < 2**19:
+        at_once *= 2
     return pl.pallas_call(
         place_kernel,
         name="place",
-        grid=(layers, owners),
-        in_specs=[pl.BlockSpec((1, 1, rows, columns), lambda l, s: (s, l, 0, 0))],
-        out_specs=pl.BlockSpec((1, rows, columns), lambda l, s: (l, s, 0)),
+        grid=(layers, owners // at_once),
+        in_specs=[pl.BlockSpec((at_once, 1, rows, columns), lambda l, s: (s, l, 0, 0))],
+        out_specs=pl.BlockSpec((1, at_once * rows, columns), lambda l, s: (l, s, 0)),
         out_shape=jax.ShapeDtypeStruct((layers, owners * rows, columns), held.dtype),
         compiler_params=pltpu.CompilerParams(vmem_limit_bytes=40 * 1024 * 1024),
         cost_estimate=pl.CostEstimate(

time: 539 us -> 531 us (0.985)
  no operation moved by 1% of the time
where the time goes in v2:
time: 531 us; the launch traced here: 530 us
  Pallas kernels  502 us (95%)
  waiting for transfers between devices  18.8 us (4%)
    pallas_call x1, Pallas kernels, exchange(): pl.pallas_call(functools.partial(exchange_kernel, groups, owners), name='...  465 us
    pallas_call x2, Pallas kernels, place(): pl.pallas_call(place_kernel, name='place', grid=(layers, owners // at_onc...  37.2 us
    all_to_all x1, waiting for transfers between devices, body(): moved = lax.all_to_all(perm, 'dev', split_axis=0, concat_axis=0, tiled=True)  18.8 us
  transfers between devices with their start and end apart: 1, of which 1 were waited for; matrix products, arithmetic and copies ran while one was open for 1% of the time, Pallas kernels for 6%

profile of v2, /device:TPU:0, one launch (start us, length us, event | category | flops | bytes accessed | tf_op | source)
XLA Modules:
  0.0 530.4 jit_solution(10196655537102388013)
XLA Ops:
  0.6 465.2 %exchange.1 = (bf16[8,2,144,9216]{3,2,1,0:T(8,128)(2,1)}, bf16[8,2,144,1024]{3,2,1,0:T(8,128)(2,1)}, f32[8,128]{1,0:T(8,128)}) custom-call(s32[64]{0:T(128)} %slot_ref.1, bf16[2,144,73728]{2,1,0:T(8,128)(2,1)} %gate_ref.1, bf16[2,144,8192]{2,1,0:T(8,128)(2,1)} %qkv_ref.1), custom_call_target="tpu_custom_call" | custom-call | bytes 84934656 | tf_op jit(solution)/shard_map/exchange/pallas_call | solution.py:227
  465.9 0.0 copy-start.3
  465.9 0.0 copy-start.4
  465.9 0.0 copy-start
  465.9 0.0 copy-start.2
  465.9 4.7 all-to-all-start
  470.7 0.0 copy-done.3
  470.7 0.1 dynamic_slice.6
  470.7 0.0 copy-done.4
  470.7 0.1 iota_compare_fusion.1
  470.8 0.1 copy.15
  470.9 0.0 copy-done
  470.9 0.1 reshape.80
  471.1 0.1 constant_dynamic-slice_fusion
  471.2 0.1 copy.16
  471.3 1.3 select_reduce_fusion
  472.6 0.1 copy.18
  472.7 0.1 mul.23
  472.8 0.0 copy-done.2
  472.8 0.1 reshape.79
  472.9 0.0 copy-start.1
  472.9 32.1 %place.3 = bf16[2,1152,9216]{2,1,0:T(8,128)(2,1)} custom-call(bf16[8,2,144,9216]{3,2,1,0:T(8,128)(2,1)} %get-tuple-element.8.in_ref), custom_call_target="tpu_custom_call" | custom-call | bytes 84934656 | tf_op jit(solution)/shard_map/place/pallas_call | solution.py:278
  505.0 0.6 sub.7
  505.6 0.0 copy-done.1
  505.6 0.1 select_reduce_fusion.1
  505.7 0.1 iota_compare_fusion
  505.8 0.1 select_reduce_fusion.2
  505.9 0.6 multiply_subtract_fusion
  506.5 18.8 %all-to-all-done.in_ref = bf16[8,2,144,1024]{3,2,1,0:T(8,128)(2,1)} async-done(((bf16[8,2,144,1024]{3,2,1,0:T(8,128)(2,1)}), bf16[8,2,144,1024]{3,2,1,0:T(8,128)(2,1)}, u32[]{:S(2)}, u32[]{:S(2)}) %all-to-all-start) | async-done | bytes 4718624 | tf_op jit(solution)/shard_map/all_to_all | solution.py:300
  525.4 5.0 place.2
  (2 shorter events, 0.0 us)
Async XLA Ops:
  465.9 4.8 copy-start.3
  465.9 4.9 copy-start.4
  465.9 5.1 copy-start
  465.9 6.9 %copy-start.2 = (f32[8,128]{1,0:T(8,128)S(1)}, f32[8,128]{1,0:T(8,128)}, u32[]{:S(2)}) copy-start(f32[8,128]{1,0:T(8,128)} %get-tuple-element.9) | copy-start | bytes 12292
  465.9 59.5 %all-to-all-start = ((bf16[8,2,144,1024]{3,2,1,0:T(8,128)(2,1)}), bf16[8,2,144,1024]{3,2,1,0:T(8,128)(2,1)}, u32[]{:S(2)}, u32[]{:S(2)}) async-start(bf16[8,2,144,1024]{3,2,1,0:T(8,128)(2,1)} %get-tuple-element.7), calls=%async_computation | async-start | bytes 9437184 | tf_op jit(solution)/shard_map/all_to_all | solution.py:300
  472.9 32.7 %copy-start.1 = (s32[46,64]{1,0:T(8,128)S(1)}, s32[46,64]{1,0:T(8,128)}, u32[]{:S(2)}) copy-start(s32[46,64]{1,0:T(8,128)} %param.10) | copy-start | bytes 35332
